TPU v7x, 512 devices: a 4x2x32 block of a 4x8x32 slice. The times are simulated.
512 devices in a mesh: groups: 2 (over y), expert: 32 (over z), tensor: 8 (over x, core).
Axes of the slice: x: 4, y: 2, z: 32, core: 2. Of those that a mesh axis runs over, the one named last changes fastest.
The devices are a block of a 4x8x32 slice.
Arguments:
- tokens: bfloat16 [8192, 7168], P(('groups', 'expert'), 'tensor'), parts along dimension 0, may hold values from -6 to 6
- choices: int32 [8192, 4], P(('groups', 'expert')), parts along dimension 0, may hold values from 0 to 15, all different within a row; in each aligned block of 128 rows (0 to 127, 128 to 255, ...) at most 48 rows name the same one
- affinity: float32 [8192, 4], P(('groups', 'expert')), parts along dimension 0, may hold values from -6 to 6
- expert_gate: bfloat16 [7168, 16384], P('tensor', 'expert'), may hold values from -0.0625 to 0.0625
- expert_up: bfloat16 [7168, 16384], P('tensor', 'expert'), may hold values from -0.0625 to 0.0625
- expert_down: bfloat16 [16384, 7168], P('expert', 'tensor'), may hold values from -0.1875 to 0.1875
- shared_in: bfloat16 [2, 1024, 7168], P(None, 'expert', 'tensor'), may hold values from -0.0625 to 0.0625
- shared_down: bfloat16 [1024, 7168], P('expert', 'tensor'), may hold values from -0.1875 to 0.1875
Outputs:
- mixed: bfloat16 [8192, 7168], P(('groups', 'expert'), 'tensor'), parts along dimension 0
There are 2 independent parts, one for each index of `groups`. A program takes and returns all parts, laid end to end along the dimension named above; an argument that names none is the same for every part. Nothing has to cross between parts.
Inputs may be any that keep to these rules, and one draw needn't show every extreme that they name: `choices`: within the rows of one index of expert (128 tokens) every expert is named at most 48 times, a bound that some block reaches; a token names 4 different experts.
All inputs are finite; a program needn't handle non-finite values.
Results may differ from a plain program's by a relative error of at most 0.02.
Values may be sent and summed in bfloat16 or wider, within the bound.
No kernel may reach another device: no remote copies, remote signals or barrier semaphores. Data moves between devices by JAX's collectives and lax.ppermute only.
A program may use at most 64 MiB of HBM per device.

v0:
```python
import jax
import jax.numpy as jnp
from jax import lax
from jax.sharding import PartitionSpec as P

FFE = 1024
EXPERTS = 16
TOP = 4
CAP = 48


def local(tokens, choices, affinity, expert_gate, expert_up, expert_down, shared_in, shared_down):
    tok_rows = tokens.shape[0]
    width_slice = tokens.shape[1]
    expert_count = lax.axis_size("expert")
    column_count = expert_gate.shape[1]
    piece_width = min(FFE, column_count)
    local_count = column_count // piece_width
    split_count = FFE // piece_width
    sigmoids = jax.nn.sigmoid(affinity)
    mix = 2.5 * sigmoids / jnp.sum(sigmoids, axis=1, keepdims=True)
    flat_ids = choices.reshape(-1)
    onehot = (flat_ids[:, None] == jnp.arange(EXPERTS, dtype=jnp.int32)[None, :]).astype(jnp.int32)
    earlier = jnp.cumsum(onehot, axis=0) - onehot
    position = jnp.sum(earlier * onehot, axis=1)
    slot_ids = flat_ids * CAP + position
    row_owner = jnp.arange(tok_rows * TOP, dtype=jnp.int32) // TOP
    source_row = jnp.zeros((EXPERTS * CAP,), jnp.int32).at[slot_ids].set(row_owner)
    filled = jnp.zeros((EXPERTS * CAP,), jnp.int32).at[slot_ids].set(1)
    packed = jnp.where(filled[:, None] > 0, tokens[source_row], jnp.zeros((), jnp.bfloat16))
    outbound = jnp.broadcast_to(
        packed.reshape(EXPERTS, 1, CAP, width_slice), (EXPERTS, split_count, CAP, width_slice)
    )
    outbound = outbound.reshape(expert_count, local_count, CAP, width_slice)
    gate_cols = expert_gate.reshape(width_slice, local_count, piece_width)
    up_cols = expert_up.reshape(width_slice, local_count, piece_width)
    down_rows = expert_down.reshape(local_count, piece_width, width_slice)
    received = lax.all_to_all(outbound, "expert", split_axis=0, concat_axis=0, tiled=True)
    gate_part = jnp.einsum(
        "nlcd,dlp->nlcp", received, gate_cols, preferred_element_type=jnp.float32
    )
    up_part = jnp.einsum("nlcd,dlp->nlcp", received, up_cols, preferred_element_type=jnp.float32)
    gate_sum = lax.psum(gate_part.astype(jnp.bfloat16), "tensor").astype(jnp.float32)
    up_sum = lax.psum(up_part.astype(jnp.bfloat16), "tensor").astype(jnp.float32)
    hidden = (jax.nn.silu(gate_sum) * up_sum).astype(jnp.bfloat16)
    produced = jnp.einsum("nlcp,lpd->nlcd", hidden, down_rows, preferred_element_type=jnp.float32)
    returned = lax.all_to_all(
        produced.astype(jnp.bfloat16), "expert", split_axis=0, concat_axis=0, tiled=True
    )
    summed = jnp.sum(
        returned.astype(jnp.float32).reshape(EXPERTS, split_count, CAP, width_slice), axis=1
    )
    picked = summed.reshape(EXPERTS * CAP, width_slice)[slot_ids].reshape(
        tok_rows, TOP, width_slice
    )
    routed = jnp.sum(mix[:, :, None] * picked, axis=1)
    terms = jnp.einsum(
        "td,gnd->gtn",
        tokens,
        lax.all_gather(shared_in, "expert", axis=1, tiled=True),
        preferred_element_type=jnp.float32,
    )
    sums = lax.psum(terms.astype(jnp.bfloat16), "tensor").astype(jnp.float32)
    shared_hidden = (jax.nn.silu(sums[0]) * sums[1]).astype(jnp.bfloat16)
    shared_out = jnp.dot(
        shared_hidden,
        lax.all_gather(shared_down, "expert", axis=0, tiled=True),
        preferred_element_type=jnp.float32,
    )
    return (routed + shared_out).astype(jnp.bfloat16)


def solution(mesh):
    placed = (
        P(("groups", "expert"), "tensor"),
        P(("groups", "expert"), None),
        P(("groups", "expert"), None),
        P("tensor", "expert"),
        P("tensor", "expert"),
        P("expert", "tensor"),
        P(None, "expert", "tensor"),
        P("expert", "tensor"),
    )
    return jax.shard_map(
        local,
        mesh=mesh,
        in_specs=placed,
        out_specs=P(("groups", "expert"), "tensor"),
        check_vma=False,
    )
```

profile of v0, /device:TPU:96, one launch (start us, length us, event | category | flops | bytes accessed | tf_op | source)
XLA Modules:
  0.0 806.6 jit_solution(5608995960913174588)
XLA Ops:
  6.5 0.0 copy-start
  6.6 0.9 copy.17
  7.4 0.1 eq.29
  7.5 0.1 eq.25
  7.6 0.7 broadcast_multiply_fusion
  8.3 1.2 reduce-window.6
  9.5 0.2 slice_reduce_fusion
  9.8 0.1 copy.16
  9.9 0.1 mul.52
  10.0 0.1 fusion.35
  10.1 2.4 scatter_custom_fusion.1
  12.6 2.4 scatter_custom_fusion
  15.1 0.1 broadcast_in_dim.33
  15.1 0.0 copy-done.1
  15.1 2.8 gather_fusion
  18.0 0.2 broadcast_select_fusion
  18.2 1.8 broadcast_in_dim.37
  20.0 44.3 %all-to-all-start = ((bf16[32,1,48,896]{3,2,1,0:T(8,128)(2,1)}), bf16[32,1,48,896]{3,2,1,0:T(8,128)(2,1)}, u32[]{:S(2)}, u32[]{:S(2)}) async-start(bf16[32,1,48,896]{3,2,1,0:T(8,128)(2,1)} %bitcast.93), calls=%async_computation | async-start | bytes 5505024 | tf_op jit(solution)/shard_map/all_to_all | solution.py:38
  64.3 0.0 copy-start.4
  64.3 0.1 all-gather.3.cloned.1.call-start
  64.4 0.7 all-gather.3.cloned.1.call-update
  65.1 0.1 all-reduce.3.cloned.1.call-start
  65.2 305.2 %all-gather.3.cloned.1.call-done = bf16[2,1024,896]{2,1,0:T(8,128)(2,1)} async-done(((bf16[2,32,896]{2,1,0:T(8,128)(2,1)}), bf16[2,1024,896]{2,1,0:T(8,128)(2,1)}) %all-gather.3.cloned.1.call-update) | async-done | bytes 3670032 | tf_op jit(solution)/shard_map/all_gather | solution.py:60
  370.4 4.0 fusion.23
  374.4 0.0 copy-start.5
  374.4 0.0 all-to-all-done
  374.4 0.0 copy-done.4
  374.4 4.8 fusion.17
  379.2 0.0 copy-done.5
  379.2 4.7 fusion.20
  383.9 0.1 all-reduce.3.cloned.1.call-update
  384.0 99.2 %all-reduce.3.cloned.1.call-done = (bf16[32,1,48,512]{3,2,0,1:T(8,128)(2,1)}, bf16[32,1,48,512]{3,2,0,1:T(8,128)(2,1)}, bf16[2,128,1024]{1,2,0:T(8,128)(2,1)}) async-done(((bf16[32,1,48,512]{3,2,0,1:T(8,128)(2,1)}, bf16[32,1,48,512]{3,2,0,1:T(8,128)(2,1)}, bf16[2,128,1024]{1,2,0:T(8,128)(2,1)}), (bf16[32,1,48,512]{3,2,0,1:T(8,128)(2,1)}, bf16[32,1,48,512]{3,2,0,1:T(8,128)(2,1)}, ...) | async-done | bytes 3670032 | tf_op jit(solution)/shard_map/psum | solution.py:44
  483.2 0.0 copy-done
  483.2 5.5 convert_bitcast_fusion
  488.7 23.4 %all-to-all-start.1 = ((bf16[32,1,48,896]{3,2,1,0:T(8,128)(2,1)}), bf16[32,1,48,896]{3,2,1,0:T(8,128)(2,1)}, u32[]{:S(2)}, u32[]{:S(2)}) async-start(bf16[32,1,48,896]{3,2,1,0:T(8,128)(2,1)} %convert_bitcast_fusion), calls=%async_computation.1 | async-start | bytes 5505024 | tf_op jit(solution)/shard_map/all_to_all | solution.py:47
  512.1 0.2 all-gather.5.cloned.1.call-start
  512.3 0.5 all-gather.5.cloned.1.call-update
  512.9 0.0 copy-done.3
  512.9 0.1 copy.15
  513.1 0.0 copy-done.2
  513.1 1.0 convert_element_type.87
  514.1 270.0 %all-to-all-done.1 = bf16[32,1,48,896]{3,2,1,0:T(8,128)(2,1)} async-done(((bf16[32,1,48,896]{3,2,1,0:T(8,128)(2,1)}), bf16[32,1,48,896]{3,2,1,0:T(8,128)(2,1)}, u32[]{:S(2)}, u32[]{:S(2)}) %all-to-all-start.1) | async-done | bytes 2752544 | tf_op jit(solution)/shard_map/all_to_all | solution.py:47
  784.1 4.0 convert_reduce_fusion
  788.2 4.4 gather_fusion.1
  792.6 1.8 reshape.107
  794.4 2.7 multiply_reduce_fusion
  797.0 0.0 all-gather.5.cloned.1.call-done
  797.1 3.0 fusion.24
  (15 shorter events, 0.1 us)
Async XLA Ops:
  6.5 476.6 %copy-start = (bf16[512,896]{1,0:T(8,128)(2,1)S(1)}, bf16[512,896]{1,0:T(8,128)(2,1)}, u32[]{:S(2)}) copy-start(bf16[512,896]{1,0:T(8,128)(2,1)} %param.13) | copy-start | bytes 2752516
  6.6 8.6 %copy-start.1 = (bf16[128,896]{1,0:T(8,128)(2,1)S(1)}, bf16[128,896]{1,0:T(8,128)(2,1)}, u32[]{:S(2)}) copy-start(bf16[128,896]{1,0:T(8,128)(2,1)} %param.8) | copy-start | bytes 688132
  20.0 354.4 %all-to-all-start = ((bf16[32,1,48,896]{3,2,1,0:T(8,128)(2,1)}), bf16[32,1,48,896]{3,2,1,0:T(8,128)(2,1)}, u32[]{:S(2)}, u32[]{:S(2)}) async-start(bf16[32,1,48,896]{3,2,1,0:T(8,128)(2,1)} %bitcast.93), calls=%async_computation | async-start | bytes 5505024 | tf_op jit(solution)/shard_map/all_to_all | solution.py:38
  64.3 310.0 %copy-start.4 = (bf16[896,512]{1,0:T(8,128)(2,1)S(1)}, bf16[896,512]{1,0:T(8,128)(2,1)}, u32[]{:S(2)}) copy-start(bf16[896,512]{1,0:T(8,128)(2,1)} %param.12) | copy-start | bytes 2752516
  64.3 306.1 %all-gather.3.cloned.1.call-start = ((), (), s32[]{:S(2)}) async-start(), calls=%async_computation.2 | async-start | bytes 3784704 | tf_op jit(solution)/shard_map/all_gather | solution.py:60
  65.1 418.0 %all-reduce.3.cloned.1.call-start = ((), (), s32[]{:S(2)}) async-start(), calls=%async_computation.4 | async-start | bytes 7340032 | tf_op jit(solution)/shard_map/psum | solution.py:44
  374.4 4.8 copy-start.5
  488.7 24.2 %copy-start.3 = (f32[128,4]{0,1:T(4,128)S(1)}, f32[128,4]{0,1:T(4,128)}, u32[]{:S(2)}) copy-start(f32[128,4]{0,1:T(4,128)} %param.10) | copy-start | bytes 6148
  488.7 24.4 %copy-start.2 = (bf16[2,128,1024]{1,2,0:T(8,128)(2,1)S(1)}, bf16[2,128,1024]{1,2,0:T(8,128)(2,1)}, u32[]{:S(2)}) copy-start(bf16[2,128,1024]{1,2,0:T(8,128)(2,1)} %get-tuple-element.7) | copy-start | bytes 1572868
  488.7 295.4 %all-to-all-start.1 = ((bf16[32,1,48,896]{3,2,1,0:T(8,128)(2,1)}), bf16[32,1,48,896]{3,2,1,0:T(8,128)(2,1)}, u32[]{:S(2)}, u32[]{:S(2)}) async-start(bf16[32,1,48,896]{3,2,1,0:T(8,128)(2,1)} %convert_bitcast_fusion), calls=%async_computation.1 | async-start | bytes 5505024 | tf_op jit(solution)/shard_map/all_to_all | solution.py:47
  512.1 285.0 %all-gather.5.cloned.1.call-start = ((), (), s32[]{:S(2)}) async-start(), calls=%async_computation.3 | async-start | bytes 1892352 | tf_op jit(solution)/shard_map/all_gather | solution.py:67
Sparse Core Ops, SparseCore 0:
  67.3 303.0 all-gather.2
  384.1 99.0 all-reduce.2
  515.0 246.0 all-gather.4
where the time goes:
time: 807 us
  waiting for transfers between devices  676 us (84%)
  starting transfers between devices  68.1 us (8%)
  matrix products  22 us (3%)
  local copies, waits for them, and re-layouts  17.5 us (2%)
  between operations  13.3 us (2%)
  other arithmetic  10 us (1%)
    all_gather x1, waiting for transfers between devices, local(): lax.all_gather(shared_in, 'expert', axis=1, tiled=True)  305 us
    all_to_all x1, waiting for transfers between devices, local(): lax.all_to_all(produced.astype(jnp.bfloat16), 'expert', split_axis=0, con...  270 us
    psum x1, waiting for transfers between devices, local(): lax.psum(up_part.astype(jnp.bfloat16), 'tensor').astype(jnp.float32)  99.2 us
    all_to_all x1, starting transfers between devices, local(): lax.all_to_all(outbound, 'expert', split_axis=0, concat_axis=0, tiled=True)  44.3 us
    all_to_all x1, starting transfers between devices, local(): lax.all_to_all(produced.astype(jnp.bfloat16), 'expert', split_axis=0, con...  23.4 us
  transfers between devices with their start and end apart: 5, of which 3 were waited for; matrix products, arithmetic and copies ran while one was open for 2% of the time, Pallas kernels for 0%

commit v1 on v0

--- a/solution.py
+++ b/solution.py
@@ -2,6 +2,7 @@
 import jax.numpy as jnp
 from jax import lax
 from jax.sharding import PartitionSpec as P
+from jax.lax import all_gather
 
 FFE = 1024
 EXPERTS = 16
@@ -41,7 +42,7 @@
     )
     up_part = jnp.einsum("nlcd,dlp->nlcp", received, up_cols, preferred_element_type=jnp.float32)
     gate_sum = lax.psum(gate_part.astype(jnp.bfloat16), "tensor").astype(jnp.float32)
-    up_sum = lax.psum(up_part.astype(jnp.bfloat16), "tensor").astype(jnp.float32)
+    up_sum = jnp.sum(all_gather(up_part.astype(jnp.bfloat16), "tensor"), 0).astype(jnp.float32)
     hidden = (jax.nn.silu(gate_sum) * up_sum).astype(jnp.bfloat16)
     produced = jnp.einsum("nlcp,lpd->nlcd", hidden, down_rows, preferred_element_type=jnp.float32)
     returned = lax.all_to_all(

time: 807 us -> 877 us (1.087)
  the two profiles are of different devices: /device:TPU:96 before, /device:TPU:166 now
where the time goes in v1:
time: 877 us; the launch traced here: 876 us
  waiting for transfers between devices  740 us (84%)
  starting transfers between devices  66.9 us (8%)
  matrix products  21.4 us (2%)
  local copies, waits for them, and re-layouts  17.4 us (2%)
  other arithmetic  17.1 us (2%)
  between operations  13.3 us (2%)
    all_to_all x1, waiting for transfers between devices, local(): lax.all_to_all(outbound, 'expert', split_axis=0, concat_axis=0, tiled=True)  270 us
    all_to_all x1, waiting for transfers between devices, local(): lax.all_to_all(produced.astype(jnp.bfloat16), 'expert', split_axis=0, con...  259 us
    psum x1, waiting for transfers between devices, local(): lax.psum(gate_part.astype(jnp.bfloat16), 'tensor').astype(jnp.float32)  93.6 us
    all_gather x1, waiting for transfers between devices, local(): all_gather(up_part.astype(jnp.bfloat16), 'tensor')  72 us
    all_to_all x1, starting transfers between devices, local(): lax.all_to_all(outbound, 'expert', split_axis=0, concat_axis=0, tiled=True)  43.1 us
    all_gather x1, waiting for transfers between devices, local(): lax.all_gather(shared_in, 'expert', axis=1, tiled=True)  28.8 us
    all_to_all x1, starting transfers between devices, local(): lax.all_to_all(produced.astype(jnp.bfloat16), 'expert', split_axis=0, con...  23.3 us
  transfers between devices with their start and end apart: 6, of which 6 were waited for; matrix products, arithmetic and copies ran while one was open for 4% of the time, Pallas kernels for 0%

profile of v1, /device:TPU:166, one launch (start us, length us, event | category | flops | bytes accessed | tf_op | source)
XLA Modules:
  0.0 875.9 jit_solution(13561633368347364298)
XLA Ops:
  6.5 0.0 copy-start
  6.6 0.9 copy.17
  7.4 0.1 eq.29
  7.5 0.1 eq.25
  7.6 0.7 broadcast_multiply_fusion
  8.3 1.2 reduce-window.6
  9.5 0.2 slice_reduce_fusion
  9.8 0.1 copy.16
  9.9 0.1 mul.52
  10.0 0.1 fusion.35
  10.1 2.4 scatter_custom_fusion.1
  12.6 2.4 scatter_custom_fusion
  15.1 0.1 broadcast_in_dim.33
  15.1 0.0 copy-done.1
  15.1 2.8 gather_fusion
  18.0 0.2 broadcast_select_fusion
  18.2 1.8 broadcast_in_dim.37
  20.0 43.1 %all-to-all-start = ((bf16[32,1,48,896]{3,2,1,0:T(8,128)(2,1)}), bf16[32,1,48,896]{3,2,1,0:T(8,128)(2,1)}, u32[]{:S(2)}, u32[]{:S(2)}) async-start(bf16[32,1,48,896]{3,2,1,0:T(8,128)(2,1)} %bitcast.105), calls=%async_computation | async-start | bytes 5505024 | tf_op jit(solution)/shard_map/all_to_all | solution.py:39
  63.1 0.1 all-gather.5.cloned.1.call-start
  63.2 0.7 all-gather.5.cloned.1.call-update
  63.9 0.1 all-gather.9.cloned.1.call-start
  64.0 270.1 %all-to-all-done = bf16[32,1,48,896]{3,2,1,0:T(8,128)(2,1)} async-done(((bf16[32,1,48,896]{3,2,1,0:T(8,128)(2,1)}), bf16[32,1,48,896]{3,2,1,0:T(8,128)(2,1)}, u32[]{:S(2)}, u32[]{:S(2)}) %all-to-all-start) | async-done | bytes 2752544 | tf_op jit(solution)/shard_map/all_to_all | solution.py:39
  334.0 0.0 copy-done.4
  334.0 4.7 fusion.17
  338.8 0.1 all-gather.9.cloned.1.call-update
  338.8 0.2 all-reduce.3.cloned.1.call-start
  339.1 28.8 %all-gather.5.cloned.1.call-done = bf16[2,1024,896]{2,1,0:T(8,128)(2,1)} async-done(((bf16[2,32,896]{2,1,0:T(8,128)(2,1)}), bf16[2,1024,896]{2,1,0:T(8,128)(2,1)}) %all-gather.5.cloned.1.call-update) | async-done | bytes 3670032 | tf_op jit(solution)/shard_map/all_gather | solution.py:61
  367.9 3.9 fusion.23
  371.8 0.0 copy-done.5
  371.8 4.7 fusion.20
  376.5 0.1 all-reduce.3.cloned.1.call-update
  376.6 72.0 %all-gather.9.cloned.1.call-done = bf16[256,1,48,512]{3,2,1,0:T(8,128)(2,1)} async-done(((bf16[32,1,48,512]{3,2,1,0:T(8,128)(2,1)}), bf16[256,1,48,512]{3,2,1,0:T(8,128)(2,1)}) %all-gather.9.cloned.1.call-update) | async-done | bytes 12582928 | tf_op jit(solution)/shard_map/all_gather | solution.py:45
  448.6 7.1 bitcast_reduce_fusion
  455.7 93.6 %all-reduce.3.cloned.1.call-done = (bf16[32,1,48,512]{3,2,0,1:T(8,128)(2,1)}, bf16[2,128,1024]{1,2,0:T(8,128)(2,1)}) async-done(((bf16[32,1,48,512]{3,2,0,1:T(8,128)(2,1)}, bf16[2,128,1024]{1,2,0:T(8,128)(2,1)}), (bf16[32,1,48,512]{3,2,0,1:T(8,128)(2,1)}, bf16[2,128,1024]{1,2,0:T(8,128)(2,1)})) %all-reduce.3.cloned.1.call-update) | async-done | bytes 2097168 | tf_op jit(solution)/shard_map/psum | solution.py:44
  549.3 5.0 convert_bitcast_fusion
  554.3 23.3 %all-to-all-start.1 = ((bf16[32,1,48,896]{3,2,1,0:T(8,128)(2,1)}), bf16[32,1,48,896]{3,2,1,0:T(8,128)(2,1)}, u32[]{:S(2)}, u32[]{:S(2)}) async-start(bf16[32,1,48,896]{3,2,1,0:T(8,128)(2,1)} %convert_bitcast_fusion), calls=%async_computation.1 | async-start | bytes 5505024 | tf_op jit(solution)/shard_map/all_to_all | solution.py:48
  577.6 0.1 all-gather.7.cloned.1.call-start
  577.7 0.6 all-gather.7.cloned.1.call-update
  578.3 0.0 copy-done.3
  578.3 0.1 copy.15
  578.5 1.0 convert_element_type.101
  579.5 259.4 %all-to-all-done.1 = bf16[32,1,48,896]{3,2,1,0:T(8,128)(2,1)} async-done(((bf16[32,1,48,896]{3,2,1,0:T(8,128)(2,1)}), bf16[32,1,48,896]{3,2,1,0:T(8,128)(2,1)}, u32[]{:S(2)}, u32[]{:S(2)}) %all-to-all-start.1) | async-done | bytes 2752544 | tf_op jit(solution)/shard_map/all_to_all | solution.py:48
  838.9 4.0 convert_reduce_fusion
  843.0 4.4 gather_fusion.1
  847.4 1.8 reshape.118
  849.2 2.7 multiply_reduce_fusion
  851.8 14.5 %all-gather.7.cloned.1.call-done = bf16[1024,896]{1,0:T(8,128)(2,1)} async-done(((bf16[32,896]{1,0:T(8,128)(2,1)}), bf16[1024,896]{1,0:T(8,128)(2,1)}) %all-gather.7.cloned.1.call-update) | async-done | bytes 1835024 | tf_op jit(solution)/shard_map/all_gather | solution.py:68
  866.3 3.0 fusion.24
  (19 shorter events, 0.1 us)
Async XLA Ops:
  6.5 542.7 %copy-start = (bf16[512,896]{1,0:T(8,128)(2,1)S(1)}, bf16[512,896]{1,0:T(8,128)(2,1)}, u32[]{:S(2)}) copy-start(bf16[512,896]{1,0:T(8,128)(2,1)} %param.13) | copy-start | bytes 2752516
  6.6 8.6 copy-start.1
  20.0 314.1 %copy-start.4 = (bf16[896,512]{1,0:T(8,128)(2,1)S(1)}, bf16[896,512]{1,0:T(8,128)(2,1)}, u32[]{:S(2)}) copy-start(bf16[896,512]{1,0:T(8,128)(2,1)} %param.12) | copy-start | bytes 2752516
  20.0 314.1 %all-to-all-start = ((bf16[32,1,48,896]{3,2,1,0:T(8,128)(2,1)}), bf16[32,1,48,896]{3,2,1,0:T(8,128)(2,1)}, u32[]{:S(2)}, u32[]{:S(2)}) async-start(bf16[32,1,48,896]{3,2,1,0:T(8,128)(2,1)} %bitcast.105), calls=%async_computation | async-start | bytes 5505024 | tf_op jit(solution)/shard_map/all_to_all | solution.py:39
  63.1 304.8 %all-gather.5.cloned.1.call-start = ((), (), s32[]{:S(2)}) async-start(), calls=%async_computation.2 | async-start | bytes 3784704 | tf_op jit(solution)/shard_map/all_gather | solution.py:61
  63.9 384.7 %all-gather.9.cloned.1.call-start = ((), (), s32[]{:S(2)}) async-start(), calls=%async_computation.4 | async-start | bytes 14155776 | tf_op jit(solution)/shard_map/all_gather | solution.py:45
  338.8 33.0 %copy-start.5 = (bf16[896,512]{1,0:T(8,128)(2,1)S(1)}, bf16[896,512]{1,0:T(8,128)(2,1)}, u32[]{:S(2)}) copy-start(bf16[896,512]{1,0:T(8,128)(2,1)} %param.11) | copy-start | bytes 2752516
  338.8 210.4 %all-reduce.3.cloned.1.call-start = ((), (), s32[]{:S(2)}) async-start(), calls=%async_computation.5 | async-start | bytes 4194304 | tf_op jit(solution)/shard_map/psum | solution.py:44
  554.3 24.0 %copy-start.3 = (f32[128,4]{0,1:T(4,128)S(1)}, f32[128,4]{0,1:T(4,128)}, u32[]{:S(2)}) copy-start(f32[128,4]{0,1:T(4,128)} %param.10) | copy-start | bytes 6148
  554.3 24.2 %copy-start.2 = (bf16[2,128,1024]{1,2,0:T(8,128)(2,1)S(1)}, bf16[2,128,1024]{1,2,0:T(8,128)(2,1)}, u32[]{:S(2)}) copy-start(bf16[2,128,1024]{1,2,0:T(8,128)(2,1)} %get-tuple-element.6) | copy-start | bytes 1572868
  554.3 284.6 %all-to-all-start.1 = ((bf16[32,1,48,896]{3,2,1,0:T(8,128)(2,1)}), bf16[32,1,48,896]{3,2,1,0:T(8,128)(2,1)}, u32[]{:S(2)}, u32[]{:S(2)}) async-start(bf16[32,1,48,896]{3,2,1,0:T(8,128)(2,1)} %convert_bitcast_fusion), calls=%async_computation.1 | async-start | bytes 5505024 | tf_op jit(solution)/shard_map/all_to_all | solution.py:48
  577.6 288.7 %all-gather.7.cloned.1.call-start = ((), (), s32[]{:S(2)}) async-start(), calls=%async_computation.3 | async-start | bytes 1892352 | tf_op jit(solution)/shard_map/all_gather | solution.py:68
Sparse Core Ops, SparseCore 0:
  66.0 301.7 all-gather.4
  370.0 78.5 all-gather.8
  451.1 98.1 all-reduce.2
  580.2 286.0 all-gather.6
